TPU v7x, 32 devices: a whole 2x2x4 slice. The times are simulated.
32 devices in a mesh: member: 8 (over y, x, core), tensor: 4 (over z).
Axes of the slice: x: 2, y: 2, z: 4, core: 2. Of those that a mesh axis runs over, the one named last changes fastest.
Arguments:
- prompt_acts: bfloat16 [128, 5120], P(None, 'member'), may hold values from -6 to 6
- gate_weight: bfloat16 [5120, 13824], P('member', 'tensor'), may hold values from -0.078125 to 0.078125
- up_weight: bfloat16 [5120, 13824], P('member', 'tensor'), may hold values from -0.078125 to 0.078125
- down_weight: bfloat16 [13824, 5120], P('tensor', 'member'), may hold values from -0.0546875 to 0.0546875
- d_table: bfloat16 [128, 3, 4, 5120], P('member'), may hold values from -6 to 6
- f_table: bfloat16 [128, 3, 4, 13824], P('member', None, None, 'tensor'), may hold values from -6 to 6
- seeds: int32 [64], P('member'), may hold values from 0 to 15
- fitness: float32 [64], P('member'), may hold values from -6 to 6
Outputs:
- outputs: bfloat16 [64, 128, 5120], P('member', None, 'tensor')
- delta_gate: bfloat16 [5120, 13824], P('member', 'tensor')
- delta_up: bfloat16 [5120, 13824], P('member', 'tensor')
- delta_down: bfloat16 [13824, 5120], P('tensor', 'member')
Inputs may be any that keep to these rules, and one draw needn't show every extreme that they name: Member m uses row (m // 8) * 16 + seeds[m] of both tables, a row in its own group's block.
All inputs are finite; a program needn't handle non-finite values.
Results may differ from a plain program's by a relative error of at most 0.025.
Values may be sent and summed in bfloat16 or wider, within the bound.
No kernel may reach another device: no remote copies, remote signals or barrier semaphores. Data moves between devices by JAX's collectives and lax.ppermute only.
A program may use at most 192 MiB of HBM per device.

v0:
```python
import math
import jax
import jax.numpy as jnp
from jax import lax
from jax.sharding import PartitionSpec as P

D = 5120
FFW = 13824
perturb_gain = 0.5


def shards(prompt_acts, gate_weight, up_weight, down_weight, d_table, f_table, seeds, fitness):
    members = seeds.shape[0]
    prompt_len = prompt_acts.shape[0]
    rank_size = d_table.shape[2]
    d_sel = jnp.take(d_table, seeds, axis=0)
    selected_factors = jnp.take(f_table, seeds, axis=0)
    d_slices = lax.all_to_all(d_sel, "member", split_axis=3, concat_axis=0, tiled=True)
    f_all, fit_all = (
        lax.all_gather(selected_factors, "member", axis=0, tiled=True),
        lax.all_gather(fitness.astype(jnp.bfloat16), "member", axis=0, tiled=True).astype(
            fitness.dtype
        ),
    )
    population = fit_all.shape[0]
    gate_part = jnp.dot(prompt_acts, gate_weight, preferred_element_type=jnp.float32)
    up_part = jnp.dot(prompt_acts, up_weight, preferred_element_type=jnp.float32)
    prompt_full = lax.all_gather(prompt_acts, "member", axis=1, tiled=True)
    gate_sum, up_sum = (
        lax.psum(gate_part.astype(jnp.bfloat16), "member").astype(jnp.float32),
        lax.psum(up_part.astype(jnp.bfloat16), "member").astype(jnp.float32),
    )
    in_factors = d_sel[:, :2].reshape(members * 2 * rank_size, D)
    proj_sum = jnp.dot(prompt_full, in_factors.T, preferred_element_type=jnp.float32)
    base_gate = gate_sum.astype(jnp.bfloat16)
    base_up = up_sum.astype(jnp.bfloat16)
    proj_inputs = (
        (proj_sum / math.sqrt(D)).astype(jnp.bfloat16).reshape(prompt_len, members, 2, rank_size)
    )
    perturbed = jnp.einsum(
        "pmkr,mkrf->mkpf", proj_inputs, selected_factors[:, :2], preferred_element_type=jnp.float32
    )
    gate = base_gate.astype(jnp.float32)[None] + perturb_gain * perturbed[:, 0]
    up = base_up.astype(jnp.float32)[None] + perturb_gain * perturbed[:, 1]
    hidden_state = (jax.nn.silu(gate) * up).astype(jnp.bfloat16)
    projection_here = jnp.einsum(
        "cdv,czv->cdz", hidden_state, selected_factors[:, 2], preferred_element_type=jnp.float32
    )
    proj_down = (lax.psum(projection_here, "tensor") / math.sqrt(FFW)).astype(jnp.bfloat16)
    hidden_rows = hidden_state.reshape(members * prompt_len, hidden_state.shape[2])
    partial_value = jnp.dot(
        hidden_rows,
        lax.all_gather(down_weight, "member", axis=1, tiled=True),
        preferred_element_type=jnp.float32,
    )
    summed = lax.psum_scatter(
        partial_value.astype(jnp.bfloat16), "tensor", scatter_dimension=1, tiled=True
    ).astype(jnp.float32)
    local_column_range = summed.shape[1]
    col_start = lax.axis_index("tensor") * local_column_range
    out_factor = lax.dynamic_slice_in_dim(d_sel[:, 2], col_start, local_column_range, 2)
    down_noise_delta = perturb_gain * jnp.einsum(
        "mpr,mrd->mpd", proj_down, out_factor, preferred_element_type=jnp.float32
    )
    outputs = (summed.reshape(members, prompt_len, local_column_range) + down_noise_delta).astype(
        jnp.bfloat16
    )
    mean = jnp.sum(fit_all) / population
    spread = jnp.sum((fit_all - mean) ** 2) / population
    score = (fit_all - mean) / jnp.sqrt(spread + 1.0)
    weighted = (d_slices.astype(jnp.float32) * score[:, None, None, None]).astype(jnp.bfloat16)
    scale = 1.0 / math.sqrt(population * rank_size)
    width_cols = weighted.shape[3]
    hidden_cols = f_all.shape[3]
    w_gate = weighted[:, 0].reshape(population * rank_size, width_cols)
    w_up = weighted[:, 1].reshape(population * rank_size, width_cols)
    w_down = weighted[:, 2].reshape(population * rank_size, width_cols)
    f_gate = f_all[:, 0].reshape(population * rank_size, hidden_cols)
    f_up = f_all[:, 1].reshape(population * rank_size, hidden_cols)
    down_factor_columns = f_all[:, 2].reshape(population * rank_size, hidden_cols)
    delta_gate = (jnp.dot(w_gate.T, f_gate, preferred_element_type=jnp.float32) * scale).astype(
        jnp.bfloat16
    )
    delta_up = (jnp.dot(w_up.T, f_up, preferred_element_type=jnp.float32) * scale).astype(
        jnp.bfloat16
    )
    delta_down = (
        jnp.dot(down_factor_columns.T, w_down, preferred_element_type=jnp.float32) * scale
    ).astype(jnp.bfloat16)
    return (outputs, delta_gate, delta_up, delta_down)


def solution(mesh):
    in_specs = (
        P(None, "member"),
        P("member", "tensor"),
        P("member", "tensor"),
        P("tensor", "member"),
        P("member", None, None, None),
        P("member", None, None, "tensor"),
        P("member"),
        P("member"),
    )
    out_specs = (
        P("member", None, "tensor"),
        P("member", "tensor"),
        P("member", "tensor"),
        P("tensor", "member"),
    )
    return jax.shard_map(shards, mesh=mesh, in_specs=in_specs, out_specs=out_specs, check_vma=False)
```

profile of v0, /device:TPU:0, one launch (start us, length us, event | category | flops | bytes accessed | tf_op | source)
XLA Modules:
  0.0 510.3 jit_solution(4729490581838769242)
XLA Ops:
  7.2 4.3 convolution_convert_fusion.1
  11.5 4.2 convolution_convert_fusion.2
  17.2 2.4 gather_fusion.1
  19.7 1.2 broadcast_select_fusion.1
  21.0 2.3 gather_fusion
  23.3 1.8 broadcast_select_fusion
  25.3 1.0 reshape.64
  26.3 52.1 %all-reduce.4.cloned.1.call-done = (bf16[128,3456]{1,0:T(8,128)(2,1)}, bf16[128,3456]{1,0:T(8,128)(2,1)}) async-done(((bf16[128,3456]{1,0:T(8,128)(2,1)}, bf16[128,3456]{1,0:T(8,128)(2,1)}), (bf16[128,3456]{1,0:T(8,128)(2,1)}, bf16[128,3456]{1,0:T(8,128)(2,1)})) %all-reduce.4.cloned.1.call-update) | async-done | bytes 1769488 | tf_op jit(solution)/shard_map/psum | solution.py:31
  78.5 1.3 convert_element_type.69
  79.8 3.1 convert_element_type.73
  82.9 21.3 %all-gather.4.cloned.1.call-done = bf16[128,5120]{1,0:T(8,128)(2,1)} async-done(((bf16[128,640]{1,0:T(8,128)(2,1)}), bf16[128,5120]{1,0:T(8,128)(2,1)}) %all-gather.4.cloned.1.call-update) | async-done | bytes 1310736 | tf_op jit(solution)/shard_map/all_gather | solution.py:28
  104.2 2.1 fusion.12
  106.2 18.7 %fusion.13 = f32[8,2,128,3456]{3,2,1,0:T(8,128)} fusion(bf16[128,8,2,4]{0,3,2,1:T(4,128)(2,1)S(1)} %bitcast.104, bf16[8,3,4,3456]{3,2,1,0:T(4,128)(2,1)} %broadcast_select_fusion.1), kind=kOutput, calls=%fused_computation.34 | convolution fusion | flops 56623104 | bytes 28770304 | tf_op jit(solution)/shard_map/pmkr,mkrf->mkpf/dot_general | solution.py:40
  125.0 11.1 %fusion = f32[8,1,128,3456]{3,2,0,1:T(8,128)} fusion(f32[8,2,128,3456]{3,2,1,0:T(8,128)} %fusion.13), kind=kLoop, calls=%fused_computation.4 | loop fusion | flops 3538944 | bytes 28311552 | tf_op jit(solution)/shard_map/mul | solution.py:43
  136.1 11.2 %slice_multiply_fusion = f32[8,1,128,3456]{3,2,1,0:T(8,128)} fusion(f32[8,2,128,3456]{3,2,1,0:T(8,128)} %fusion.13), kind=kLoop, calls=%fused_computation.2 | loop fusion | flops 3538944 | bytes 28311552 | tf_op jit(solution)/shard_map/mul | solution.py:44
  147.3 13.3 %fusion.4 = bf16[1024,3456]{1,0:T(8,128)(2,1)} fusion(f32[8,1,128,3456]{3,2,1,0:T(8,128)} %slice_multiply_fusion, f32[8,1,128,3456]{3,2,0,1:T(8,128)} %fusion, f32[128,3456]{1,0:T(8,128)} %convert_element_type.73, f32[128,3456]{1,0:T(8,128)S(1)} %convert_element_type.69), kind=kLoop, calls=%fused_computation.11 | loop fusion | flops 28311552 | bytes 38928384 | tf_op jit(solution)/shard_map/convert_element_type | solution.py:45
  160.6 114.7 %all-gather.6.cloned.1.call-done = bf16[3456,5120]{1,0:T(8,128)(2,1)} async-done(((bf16[3456,640]{1,0:T(8,128)(2,1)}), bf16[3456,5120]{1,0:T(8,128)(2,1)}) %all-gather.6.cloned.1.call-update) | async-done | bytes 35389456 | tf_op jit(solution)/shard_map/all_gather | solution.py:53
  275.2 45.1 %convolution_convert_fusion = bf16[1024,5120]{1,0:T(8,128)(2,1)} fusion(bf16[1024,3456]{1,0:T(8,128)(2,1)} %fusion.4, bf16[3456,5120]{1,0:T(8,128)(2,1)} %all-gather.6.cloned.1.call-done), kind=kOutput, calls=%fused_computation.13 | convolution fusion | flops 36244029440 | bytes 52953088 | tf_op jit(solution)/shard_map/dot_general | solution.py:51
  320.4 14.9 %copy.34 = bf16[8,3,4,5120]{0,2,1,3:T(4,128)(2,1)} copy(bf16[8,3,4,5120]{3,2,1,0:T(4,128)(2,1)S(1)} %broadcast_select_fusion) | data formatting | bytes 1966080 | tf_op jit(solution)/shard_map/jit(_take)/select_n | solution.py:16
  335.3 19.3 %reshape.104 = bf16[8,2,30720]{2,1,0:T(2,128)(2,1)} reshape(bf16[5120,3,4,8]{3,2,1,0:T(4,128)(2,1)} %bitcast.102) | data formatting | bytes 1966080
  354.6 3.6 all-to-all-start
  359.8 19.9 %all-reduce = bf16[64]{0:T(256)(128)(2,1)S(1)} all-reduce(bf16[64]{0:T(256)(128)(2,1)S(1)} %dynamic-update-slice), channel_id=1, replica_groups=mesh['member'=8,'tensor'=4] {'member'}, use_global_device_ids=true, to_apply=%add | all-reduce | flops 64 | bytes 256
  382.3 19.7 %reshape.105 = bf16[5120,3,4,8]{3,2,1,0:T(4,128)(2,1)} reshape(bf16[8,2,30720]{2,1,0:T(2,128)(2,1)S(1)} %all-to-all-done) | data formatting | bytes 1966080
  402.1 19.0 %copy.35 = f32[8,3,4,8,640]{4,0,3,2,1:T(8,128)S(1)} copy(bf16[8,3,4,8,640]{0,2,1,4,3:T(4,128)(2,1)} %bitcast.101) | data formatting | bytes 2949120 | tf_op jit(solution)/shard_map/convert_element_type | solution.py:71
  421.4 13.1 %fusion.8 = f32[8,128,4]{1,2,0:T(4,128)S(1)} fusion(f32[128,3456]{1,0:T(8,128)} %convert_element_type.73, f32[128,3456]{1,0:T(8,128)} %copy-done.3, bf16[8,3,4,3456]{3,2,1,0:T(4,128)(2,1)} %broadcast_select_fusion.1, f32[8,2,128,3456]{3,2,1,0:T(8,128)} %fusion.13), kind=kOutput, calls=%fused_computation.20 | convolution fusion | flops 63700992 | bytes 32088064 | tf_op jit(solution)/shard_map/cdv,czv->cdz/dot_general | solution.py:46
  434.4 20.0 %psum.23 = f32[8,128,4]{1,2,0:T(4,128)S(1)} all-reduce(f32[8,128,4]{1,2,0:T(4,128)S(1)} %fusion.8), channel_id=1, replica_groups=mesh['member'=8,'tensor'=4] {'tensor'}, use_global_device_ids=true, to_apply=%region_3.4 | all-reduce | flops 4096 | bytes 32768 | tf_op jit(solution)/shard_map/psum | solution.py:49
  454.4 3.6 fusion.23
  458.1 3.5 fusion.6
  461.5 3.5 fusion.7
  465.0 3.7 fusion.5
  468.7 30.9 %reduce-scatter.2.cloned.1.call-done = bf16[1024,1280]{1,0:T(8,128)(2,1)} async-done(((bf16[1024,5120]{1,0:T(8,128)(2,1)}), bf16[1024,1280]{1,0:T(8,128)(2,1)}) %reduce-scatter.2.cloned.1.call-update) | async-done | bytes 2621456 | tf_op jit(solution)/shard_map/reduce_scatter | solution.py:56
  499.6 4.2 fusion.10
  (40 shorter events, 4.4 us)
Async XLA Ops:
  7.2 13.8 %copy-start = (bf16[16,3,4,5120]{3,2,1,0:T(4,128)(2,1)S(1)}, bf16[16,3,4,5120]{3,2,1,0:T(4,128)(2,1)}, u32[]{:S(2)}) copy-start(bf16[16,3,4,5120]{3,2,1,0:T(4,128)(2,1)} %param.12) | copy-start | bytes 5898244
  7.2 71.3 %all-reduce.4.cloned.1.call-start = ((), (), s32[]{:S(2)}) async-start(), calls=%async_computation.6 | async-start | bytes 3538944 | tf_op jit(solution)/shard_map/psum | solution.py:31
  11.5 5.7 %copy-start.4 = (s32[8]{0:T(128)S(1)}, s32[8]{0:T(128)}, u32[]{:S(2)}) copy-start(s32[8]{0:T(128)} %param.14) | copy-start | bytes 100
  15.7 88.5 %all-gather.4.cloned.1.call-start = ((), (), s32[]{:S(2)}) async-start(), calls=%async_computation.2 | async-start | bytes 1474560 | tf_op jit(solution)/shard_map/all_gather | solution.py:28
  16.4 258.8 %all-gather.6.cloned.1.call-start = ((), (), s32[]{:S(2)}) async-start(), calls=%async_computation.3 | async-start | bytes 39813120 | tf_op jit(solution)/shard_map/all_gather | solution.py:53
  17.2 437.3 %all-gather.8.cloned.1.call-start = ((), (), s32[]{:S(2)}) async-start(), calls=%async_computation.5 | async-start | bytes 5971968 | tf_op jit(solution)/shard_map/all_gather | solution.py:20
  20.9 478.7 %reduce-scatter.2.cloned.1.call-start = ((), (), s32[]{:S(2)}) async-start(), calls=%async_computation.4 | async-start | bytes 13107200 | tf_op jit(solution)/shard_map/reduce_scatter | solution.py:56
  25.1 333.1 %copy-start.2 = (bf16[8,3,4,5120]{3,2,1,0:T(4,128)(2,1)}, bf16[8,3,4,5120]{3,2,1,0:T(4,128)(2,1)S(1)}, u32[]{:S(2)}) copy-start(bf16[8,3,4,5120]{3,2,1,0:T(4,128)(2,1)S(1)} %broadcast_select_fusion) | copy-start | bytes 2949124
  79.8 67.5 %copy-start.3 = (f32[128,3456]{1,0:T(8,128)}, f32[128,3456]{1,0:T(8,128)S(1)}, u32[]{:S(2)}) copy-start(f32[128,3456]{1,0:T(8,128)S(1)} %convert_element_type.69) | copy-start | bytes 5308420
  335.3 22.9 %copy-start.5 = (f32[8]{0:T(128)S(1)}, f32[8]{0:T(128)}, u32[]{:S(2)}) copy-start(f32[8]{0:T(128)} %param.15) | copy-start | bytes 100
  335.3 22.9 %copy-start.6 = (u32[32]{0:T(128)S(1)}, u32[32]{0:T(128)}, u32[]{:S(2)}) copy-start(u32[32]{0:T(128)} %constant.62) | copy-start | bytes 388
  354.6 27.7 %all-to-all-start = ((bf16[8,2,30720]{2,1,0:T(2,128)(2,1)}), bf16[8,2,30720]{2,1,0:T(2,128)(2,1)S(1)}, u32[]{:S(2)}, u32[]{:S(2)}) async-start(bf16[8,2,30720]{2,1,0:T(2,128)(2,1)} %reshape.104), calls=%async_computation.1 | async-start | bytes 1966080 | tf_op jit(solution)/shard_map/all_to_all | solution.py:18
  465.0 34.6 %slice-start = ((bf16[8,3,4,5120]{3,2,1,0:T(4,128)(2,1)}), bf16[8,1,4,5120]{3,2,1,0:T(4,128)(2,1)S(1)}, s32[]{:S(2)}) async-start(bf16[8,3,4,5120]{3,2,1,0:T(4,128)(2,1)} %copy-done.2), calls=%async_computation.7 | async-start | bytes 655360 | tf_op jit(solution)/shard_map/slice | solution.py:61
  465.0 38.8 %copy-start.1 = (bf16[16,3,4,5120]{3,2,1,0:T(4,128)(2,1)S(1)}, bf16[16,3,4,5120]{3,2,1,0:T(4,128)(2,1)}, u32[]{:S(2)}) copy-start(bf16[16,3,4,5120]{3,2,1,0:T(4,128)(2,1)} %param.12) | copy-start | bytes 5898244
Sparse Core Ops, SparseCore 0:
  15.8 62.6 all-reduce.3
  80.4 23.7 all-gather.3
  106.1 169.1 all-gather.5
  277.5 41.2 all-gather.7
  321.1 178.5 reduce-scatter.1
where the time goes:
time: 511 us; the launch traced here: 510 us
  waiting for transfers between devices  220 us (43%)
  matrix products  102 us (20%)
  local copies, waits for them, and re-layouts  83.5 us (16%)
  other arithmetic  44.6 us (9%)
  blocking collectives  39.9 us (8%)
  between operations  15.9 us (3%)
    all_gather x1, waiting for transfers between devices, shards(): lax.all_gather(down_weight, 'member', axis=1, tiled=True)  115 us
    psum x1, waiting for transfers between devices, shards(): lax.psum(up_part.astype(jnp.bfloat16), 'member').astype(jnp.float32)  52.1 us
    dot_general x1, matrix products, shards(): jnp.dot(hidden_rows, lax.all_gather(down_weight, 'member', axis=1, tiled=...  45.1 us
    unnamed x19, local copies, waits for them, and re-layouts  40 us
    reduce_scatter x1, waiting for transfers between devices, shards(): lax.psum_scatter(partial_value.astype(jnp.bfloat16), 'tensor', scatter_di...  30.9 us
    all_gather x1, waiting for transfers between devices, shards(): prompt_full = lax.all_gather(prompt_acts, 'member', axis=1, tiled=True)  21.3 us
    psum x1, blocking collectives, shards(): lax.psum(projection_here, 'tensor') / math.sqrt(FFW)  20 us
    unnamed x1, blocking collectives  19.9 us
  transfers between devices with their start and end apart: 6, of which 4 were waited for; matrix products, arithmetic and copies ran while one was open for 43% of the time, Pallas kernels for 0%

commit v1 on v0

--- a/solution.py
+++ b/solution.py
@@ -50,7 +50,10 @@
     hidden_rows = hidden_state.reshape(members * prompt_len, hidden_state.shape[2])
     partial_value = jnp.dot(
         hidden_rows,
-        lax.all_gather(down_weight, "member", axis=1, tiled=True),
+        jnp.concatenate(
+            lax.all_to_all(jnp.stack([down_weight] * lax.axis_size("member")), "member", 0, 0),
+            axis=1,
+        ),
         preferred_element_type=jnp.float32,
     )
     summed = lax.psum_scatter(

time: 511 us -> 701 us (1.37)
  waiting for transfers between devices: 220 us -> 416 us
  other arithmetic: 44.6 us -> 21.3 us
  local copies, waits for them, and re-layouts: 83.5 us -> 104 us
  matrix products: 102 us -> 90.4 us
  starting transfers between devices: 3.75 us -> 11.1 us
    psum x1, waiting for transfers between devices: 52.1 us -> 310 us  [shards(): lax.psum(up_part.astype(jnp.bfloat16), 'member').astype(jnp.float32)]
    all_gather x1 -> x0, waiting for transfers between devices: 115 us -> none  [shards(): lax.all_gather(down_weight, 'member', axis=1, tiled=True)]
    all_to_all x0 -> x1, waiting for transfers between devices: none -> 39.1 us  [shards(): lax.all_to_all(jnp.stack([down_weight] * lax.axis_size('member')), 'membe...]
    mul x2 -> x0, other arithmetic: 22.2 us -> none  [the longest x1 11.2 us: shards(): up = base_up.astype(jnp.float32)[None] + perturb_gain * perturbed[:, 1]]
    another operation x0 -> x1, local copies, waits for them, and re-layouts: none -> 13.4 us  [shards(): jnp.stack([down_weight] * lax.axis_size('member'))]
    dot_general x1, matrix products: 13.1 us -> 5.08 us  [shards(): jnp.einsum('cdv,czv->cdz', hidden_state, selected_factors[:, 2], preferre...]
    all_to_all x0 -> x1, starting transfers between devices: none -> 7.36 us  [shards(): lax.all_to_all(jnp.stack([down_weight] * lax.axis_size('member')), 'membe...]
    unnamed x19 -> x22, local copies, waits for them, and re-layouts: 40 us -> 47.2 us
  transfers between devices with their start and end apart: 6 -> 6, of which waited for: 4 -> 4; matrix products, arithmetic and copies ran while one was open for 43% -> 27% of each run, Pallas kernels for 0% -> 0%
where the time goes in v1:
time: 701 us; the launch traced here: 700 us
  waiting for transfers between devices  416 us (59%)
  local copies, waits for them, and re-layouts  104 us (15%)
  matrix products  90.4 us (13%)
  blocking collectives  40.8 us (6%)
  other arithmetic  21.3 us (3%)
  between operations  16 us (2%)
  starting transfers between devices  11.1 us (2%)
    psum x1, waiting for transfers between devices, shards(): lax.psum(up_part.astype(jnp.bfloat16), 'member').astype(jnp.float32)  310 us
    unnamed x22, local copies, waits for them, and re-layouts  47.2 us
    dot_general x1, matrix products, shards(): jnp.dot(hidden_rows, jnp.concatenate(lax.all_to_all(jnp.stack([down_weigh...  45.3 us
    all_to_all x1, waiting for transfers between devices, shards(): lax.all_to_all(jnp.stack([down_weight] * lax.axis_size('member')), 'membe...  39.1 us
    reduce_scatter x1, waiting for transfers between devices, shards(): lax.psum_scatter(partial_value.astype(jnp.bfloat16), 'tensor', scatter_di...  37.7 us
    all_gather x1, waiting for transfers between devices, shards(): prompt_full = lax.all_gather(prompt_acts, 'member', axis=1, tiled=True)  28.2 us
    psum x1, blocking collectives, shards(): lax.psum(projection_here, 'tensor') / math.sqrt(FFW)  20.9 us
    unnamed x1, blocking collectives  19.9 us
  transfers between devices with their start and end apart: 6, of which 4 were waited for; matrix products, arithmetic and copies ran while one was open for 27% of the time, Pallas kernels for 0%

profile of v1, /device:TPU:0, one launch (start us, length us, event | category | flops | bytes accessed | tf_op | source)
XLA Modules:
  0.0 699.8 jit_solution(15387109361979708764)
XLA Ops:
  7.2 7.3 %copy.43 = bf16[3456,640]{0,1:T(8,128)(2,1)} copy(bf16[3456,640]{1,0:T(8,128)(2,1)} %param.11) | data formatting | bytes 8847360 | tf_op args[3]
  14.5 13.4 %stack.2 = bf16[8,3456,640]{1,2,0:T(8,128)(2,1)} broadcast(bf16[3456,640]{0,1:T(8,128)(2,1)} %copy.43), dimensions={1,2} | broadcast | bytes 39813120 | tf_op jit(solution)/shard_map/stack | solution.py:54
  27.9 7.4 %all-to-all-start = ((bf16[8,3456,640]{1,2,0:T(8,128)(2,1)}), bf16[8,3456,640]{1,2,0:T(8,128)(2,1)}, u32[]{:S(2)}, u32[]{:S(2)}) async-start(bf16[8,3456,640]{1,2,0:T(8,128)(2,1)} %stack.2), calls=%async_computation | async-start | bytes 70778880 | tf_op jit(solution)/shard_map/all_to_all | solution.py:54
  35.4 4.0 convolution_convert_fusion.1
  39.4 4.1 convolution_convert_fusion.2
  44.3 2.4 gather_fusion.1
  46.8 1.2 broadcast_select_fusion.1
  48.1 2.3 gather_fusion
  50.4 1.7 broadcast_select_fusion
  53.3 310.3 %all-reduce.4.cloned.1.call-done = (bf16[128,3456]{1,0:T(8,128)(2,1)}, bf16[128,3456]{1,0:T(8,128)(2,1)}) async-done(((bf16[128,3456]{1,0:T(8,128)(2,1)}, bf16[128,3456]{1,0:T(8,128)(2,1)}), (bf16[128,3456]{1,0:T(8,128)(2,1)}, bf16[128,3456]{1,0:T(8,128)(2,1)})) %all-reduce.4.cloned.1.call-update) | async-done | bytes 1769488 | tf_op jit(solution)/shard_map/psum | solution.py:31
  363.6 1.3 convert_element_type.80
  364.9 2.5 convert_element_type.76
  367.3 28.2 %all-gather.3.cloned.1.call-done = bf16[128,5120]{1,0:T(8,128)(2,1)} async-done(((bf16[128,640]{1,0:T(8,128)(2,1)}), bf16[128,5120]{1,0:T(8,128)(2,1)}) %all-gather.3.cloned.1.call-update) | async-done | bytes 1310736 | tf_op jit(solution)/shard_map/all_gather | solution.py:28
  395.5 2.1 fusion.12
  397.6 15.0 %fusion.13 = f32[8,2,128,3456]{3,2,1,0:T(8,128)} fusion(bf16[128,8,2,4]{0,3,2,1:T(4,128)(2,1)S(1)} %bitcast.96, bf16[8,3,4,3456]{3,2,1,0:T(4,128)(2,1)} %broadcast_select_fusion.1), kind=kOutput, calls=%fused_computation.31 | convolution fusion | flops 56623104 | bytes 28770304 | tf_op jit(solution)/shard_map/pmkr,mkrf->mkpf/dot_general | solution.py:40
  412.6 13.2 %fusion.3 = bf16[8,128,3456]{2,1,0:T(8,128)(2,1)} fusion(f32[8,2,128,3456]{3,2,1,0:T(8,128)} %fusion.13, f32[128,3456]{1,0:T(8,128)S(1)} %convert_element_type.80, f32[128,3456]{1,0:T(8,128)S(1)} %copy-done.3), kind=kLoop, calls=%fused_computation.6 | loop fusion | flops 35389440 | bytes 38928384 | tf_op jit(solution)/shard_map/convert_element_type | solution.py:45
  425.9 39.1 %all-to-all-done = bf16[8,3456,640]{1,2,0:T(8,128)(2,1)} async-done(((bf16[8,3456,640]{1,2,0:T(8,128)(2,1)}), bf16[8,3456,640]{1,2,0:T(8,128)(2,1)}, u32[]{:S(2)}, u32[]{:S(2)}) %all-to-all-start) | async-done | bytes 35389472 | tf_op jit(solution)/shard_map/all_to_all | solution.py:54
  464.9 45.3 %convolution_convert_fusion = bf16[1024,5120]{1,0:T(8,128)(2,1)} fusion(bf16[1024,3456]{1,0:T(8,128)(2,1)} %bitcast.94, bf16[3456,5120]{0,1:T(8,128)(2,1)} %bitcast.7), kind=kOutput, calls=%fused_computation.11 | convolution fusion | flops 36244029440 | bytes 52953088 | tf_op jit(solution)/shard_map/dot_general | solution.py:51
  510.2 14.9 %copy.44 = bf16[8,3,4,5120]{0,2,1,3:T(4,128)(2,1)} copy(bf16[8,3,4,5120]{3,2,1,0:T(4,128)(2,1)S(1)} %broadcast_select_fusion) | data formatting | bytes 1966080 | tf_op jit(solution)/shard_map/jit(_take)/select_n | solution.py:16
  525.2 19.3 %reshape.134 = bf16[8,2,30720]{2,1,0:T(2,128)(2,1)} reshape(bf16[5120,3,4,8]{3,2,1,0:T(4,128)(2,1)} %bitcast.93) | data formatting | bytes 1966080
  544.5 3.6 all-to-all-start.1
  549.6 19.9 %all-reduce = bf16[64]{0:T(256)(128)(2,1)S(1)} all-reduce(bf16[64]{0:T(256)(128)(2,1)S(1)} %dynamic-update-slice), channel_id=1, replica_groups=mesh['member'=8,'tensor'=4] {'member'}, use_global_device_ids=true, to_apply=%add | all-reduce | flops 64 | bytes 256
  572.1 19.7 %reshape.135 = bf16[5120,3,4,8]{3,2,1,0:T(4,128)(2,1)} reshape(bf16[8,2,30720]{2,1,0:T(2,128)(2,1)S(1)} %all-to-all-done.1) | data formatting | bytes 1966080
  591.8 19.0 %copy.45 = f32[8,3,4,8,640]{4,0,3,2,1:T(8,128)S(1)} copy(bf16[8,3,4,8,640]{0,2,1,4,3:T(4,128)(2,1)} %bitcast.92) | data formatting | bytes 2949120 | tf_op jit(solution)/shard_map/convert_element_type | solution.py:74
  611.1 5.1 fusion.15
  616.2 20.9 %psum.23 = f32[8,128,4]{1,2,0:T(4,128)S(1)} all-reduce(f32[8,128,4]{1,2,0:T(4,128)S(1)} %fusion.15), channel_id=1, replica_groups=mesh['member'=8,'tensor'=4] {'tensor'}, use_global_device_ids=true, to_apply=%region_3.4 | all-reduce | flops 4096 | bytes 32768 | tf_op jit(solution)/shard_map/psum | solution.py:49
  637.1 3.7 fusion.22
  640.7 3.5 fusion.9
  644.2 3.5 fusion.8
  647.7 3.7 fusion.7
  651.4 37.7 %reduce-scatter.2.cloned.1.call-done = bf16[1024,1280]{1,0:T(8,128)(2,1)} async-done(((bf16[1024,5120]{1,0:T(8,128)(2,1)}), bf16[1024,1280]{1,0:T(8,128)(2,1)}) %reduce-scatter.2.cloned.1.call-update) | async-done | bytes 2621456 | tf_op jit(solution)/shard_map/reduce_scatter | solution.py:59
  689.1 4.2 fusion.10
  (41 shorter events, 4.5 us)
Async XLA Ops:
  7.2 40.9 %copy-start = (bf16[16,3,4,5120]{3,2,1,0:T(4,128)(2,1)S(1)}, bf16[16,3,4,5120]{3,2,1,0:T(4,128)(2,1)}, u32[]{:S(2)}) copy-start(bf16[16,3,4,5120]{3,2,1,0:T(4,128)(2,1)} %param.12) | copy-start | bytes 5898244
  27.9 7.4 %copy-start.4 = (bf16[128,640]{1,0:T(8,128)(2,1)S(1)}, bf16[128,640]{1,0:T(8,128)(2,1)}, u32[]{:S(2)}) copy-start(bf16[128,640]{1,0:T(8,128)(2,1)} %param.8) | copy-start | bytes 491524
  27.9 437.0 %all-to-all-start = ((bf16[8,3456,640]{1,2,0:T(8,128)(2,1)}), bf16[8,3456,640]{1,2,0:T(8,128)(2,1)}, u32[]{:S(2)}, u32[]{:S(2)}) async-start(bf16[8,3456,640]{1,2,0:T(8,128)(2,1)} %stack.2), calls=%async_computation | async-start | bytes 70778880 | tf_op jit(solution)/shard_map/all_to_all | solution.py:54
  35.3 328.3 %all-reduce.4.cloned.1.call-start = ((), (), s32[]{:S(2)}) async-start(), calls=%async_computation.6 | async-start | bytes 3538944 | tf_op jit(solution)/shard_map/psum | solution.py:31
  39.4 4.9 copy-start.5
  43.5 352.0 %all-gather.3.cloned.1.call-start = ((), (), s32[]{:S(2)}) async-start(), calls=%async_computation.3 | async-start | bytes 1474560 | tf_op jit(solution)/shard_map/all_gather | solution.py:28
  44.3 592.8 %all-gather.5.cloned.1.call-start = ((), (), s32[]{:S(2)}) async-start(), calls=%async_computation.5 | async-start | bytes 5971968 | tf_op jit(solution)/shard_map/all_gather | solution.py:20
  48.0 641.1 %reduce-scatter.2.cloned.1.call-start = ((), (), s32[]{:S(2)}) async-start(), calls=%async_computation.4 | async-start | bytes 13107200 | tf_op jit(solution)/shard_map/reduce_scatter | solution.py:59
  52.1 496.0 %copy-start.2 = (bf16[8,3,4,5120]{3,2,1,0:T(4,128)(2,1)}, bf16[8,3,4,5120]{3,2,1,0:T(4,128)(2,1)S(1)}, u32[]{:S(2)}) copy-start(bf16[8,3,4,5120]{3,2,1,0:T(4,128)(2,1)S(1)} %broadcast_select_fusion) | copy-start | bytes 2949124
  397.6 15.0 %copy-start.3 = (f32[128,3456]{1,0:T(8,128)S(1)}, f32[128,3456]{1,0:T(8,128)}, u32[]{:S(2)}) copy-start(f32[128,3456]{1,0:T(8,128)} %convert_element_type.76) | copy-start | bytes 5308420
  525.2 22.9 %copy-start.6 = (f32[8]{0:T(128)S(1)}, f32[8]{0:T(128)}, u32[]{:S(2)}) copy-start(f32[8]{0:T(128)} %param.15) | copy-start | bytes 100
  525.2 22.9 %copy-start.7 = (u32[32]{0:T(128)S(1)}, u32[32]{0:T(128)}, u32[]{:S(2)}) copy-start(u32[32]{0:T(128)} %constant.62) | copy-start | bytes 388
  544.5 27.6 %all-to-all-start.1 = ((bf16[8,2,30720]{2,1,0:T(2,128)(2,1)}), bf16[8,2,30720]{2,1,0:T(2,128)(2,1)S(1)}, u32[]{:S(2)}, u32[]{:S(2)}) async-start(bf16[8,2,30720]{2,1,0:T(2,128)(2,1)} %reshape.134), calls=%async_computation.2 | async-start | bytes 1966080 | tf_op jit(solution)/shard_map/all_to_all | solution.py:18
  647.7 41.4 %slice-start = ((bf16[8,3,4,5120]{3,2,1,0:T(4,128)(2,1)}), bf16[8,1,4,5120]{3,2,1,0:T(4,128)(2,1)S(1)}, s32[]{:S(2)}) async-start(bf16[8,3,4,5120]{3,2,1,0:T(4,128)(2,1)} %copy-done.2), calls=%async_computation.7 | async-start | bytes 655360 | tf_op jit(solution)/shard_map/slice | solution.py:64
  647.7 45.6 %copy-start.1 = (bf16[16,3,4,5120]{3,2,1,0:T(4,128)(2,1)S(1)}, bf16[16,3,4,5120]{3,2,1,0:T(4,128)(2,1)}, u32[]{:S(2)}) copy-start(bf16[16,3,4,5120]{3,2,1,0:T(4,128)(2,1)} %param.12) | copy-start | bytes 5898244
Sparse Core Ops, SparseCore 0:
  43.6 319.8 all-reduce.3
  365.5 29.9 all-gather.2
  398.0 62.7 all-gather.4
  510.4 178.7 reduce-scatter.1
